TPU v7x, 32 devices: a whole 2x2x4 slice. The times are simulated.
32 devices in a mesh: samp: 8 (over y, x, core), snp: 4 (over z).
Axes of the slice: x: 2, y: 2, z: 4, core: 2. Of those that a mesh axis runs over, the one named last changes fastest.
Arguments:
- genotypes: bfloat16 [8192, 16384], P('samp', 'snp'), may hold values from -6 to 6
- probes: bfloat16 [8, 8192], P(None, 'samp'), may hold values from -6 to 6
- env_label: int32 [8192], P('samp'), may hold values from 0 to 7
- variances: float32 [3], replicated, may hold values from 0.25 to 1
Outputs:
- first: float32 [8, 8192], P(None, 'samp')
- second: float32 [8, 8192], P(None, 'samp')
All inputs are finite; a program needn't handle non-finite values.
Results may differ from a plain program's by a relative error of at most 0.0018.
Values may be sent and summed in bfloat16 or wider, within the bound.
No kernel may reach another device: no remote copies, remote signals or barrier semaphores. Data moves between devices by JAX's collectives and lax.ppermute only.
A program may use at most 64 MiB of HBM per device.

v0:
```python
import jax
import jax.numpy as jnp
from jax import lax
from jax.sharding import PartitionSpec as P

SNPS = 16384
PROBES = 8
ENVS = 8


def local_image(snp_panel, genotypes):
    return lax.dot_general(
        snp_panel, genotypes, (((1,), (1,)), ((), ())), preferred_element_type=jnp.float32
    )


def apply_operator(current, genotypes, onehot, variances):
    rounded = current.astype(jnp.bfloat16)
    scaled = (onehot[:, None, :] * rounded[None, :, :]).reshape(ENVS * PROBES, -1)
    panel = jnp.concatenate([rounded, scaled], axis=0)
    partial_panel = jnp.dot(panel, genotypes, preferred_element_type=jnp.float32)
    snp_panel = lax.psum(partial_panel, "samp").astype(jnp.bfloat16)
    image = local_image(snp_panel, genotypes)
    additive = image[:PROBES]
    blocks = image[PROBES:].reshape(ENVS, PROBES, -1)
    interaction = jnp.sum(onehot.astype(jnp.float32)[:, None, :] * blocks, axis=0)
    weighted = variances[0] * additive / SNPS + variances[1] * interaction / SNPS
    totals = lax.psum(weighted, "snp")
    return totals + variances[2] * current


def per_device(genotypes, probes, env_label, variances):
    labels = jnp.arange(ENVS, dtype=jnp.int32)
    onehot = (env_label[None, :] == labels[:, None]).astype(jnp.bfloat16)
    first = apply_operator(probes.astype(jnp.float32), genotypes, onehot, variances)
    second = apply_operator(first, genotypes, onehot, variances)
    return (first, second)


def solution(mesh):
    return jax.shard_map(
        per_device,
        mesh=mesh,
        in_specs=(P("samp", "snp"), P(None, "samp"), P("samp"), P()),
        out_specs=(P(None, "samp"), P(None, "samp")),
        check_vma=False,
    )
```

profile of v0, /device:TPU:0, one launch (start us, length us, event | category | flops | bytes accessed | tf_op | source)
XLA Modules:
  0.0 167.7 jit_solution(6879203342592267592)
XLA Ops:
  0.6 1.4 fusion.25
  2.1 0.7 fusion.21
  2.8 0.7 multiply_bitcast_fusion.1
  3.5 5.0 %fusion.8 = f32[72,4096]{1,0:T(8,128)S(1)} fusion(bf16[1024,4096]{1,0:T(8,128)(2,1)} %param.4, bf16[64,1024]{1,0:T(8,128)(2,1)S(1)} %multiply_bitcast_fusion.1, bf16[8,1024]{1,0:T(8,128)(2,1)} %param.5), kind=kOutput, calls=%fused_computation.10 | convolution fusion | flops 604274688 | bytes 9715712 | tf_op jit(solution)/shard_map/dot_general | solution.py:21
  8.5 0.0 copy-start
  8.5 53.0 %all-reduce.2 = bf16[72,4096]{1,0:T(8,128)(2,1)S(1)} all-reduce(f32[72,4096]{1,0:T(8,128)S(1)} %fusion.8), channel_id=1, replica_groups=mesh['samp'=8,'snp'=4] {'samp'}, use_global_device_ids=true, to_apply=%region_0.0 | all-reduce | flops 294912 | bytes 1769472 | tf_op jit(solution)/shard_map/psum | solution.py:22
  61.5 6.0 %fusion.27 = f32[72,1024]{1,0:T(8,128)S(1)} fusion(bf16[72,4096]{1,0:T(8,128)(2,1)S(1)} %all-reduce.2, bf16[1024,4096]{1,0:T(8,128)(2,1)} %param.4), kind=kOutput, calls=%fused_computation.36 | convolution fusion | flops 603979776 | bytes 9273344 | tf_op jit(solution)/shard_map/dot_general | solution.py:12
  67.6 1.2 fusion.19
  68.8 19.5 %psum.29 = f32[8,1024]{1,0:T(8,128)S(1)} all-reduce(f32[8,1024]{1,0:T(8,128)S(1)} %fusion.19), channel_id=1, replica_groups=mesh['samp'=8,'snp'=4] {'snp'}, use_global_device_ids=true, to_apply=%region_2.0 | all-reduce | flops 8192 | bytes 65536 | tf_op jit(solution)/shard_map/psum | solution.py:28
  88.3 0.0 copy-done
  88.3 0.7 fusion.24
  89.0 0.0 copy-start.1
  89.1 5.0 %fusion.12 = f32[72,4096]{1,0:T(8,128)S(1)} fusion(bf16[1024,4096]{1,0:T(8,128)(2,1)} %param.4, bf16[64,1024]{1,0:T(8,128)(2,1)S(1)} %multiply_bitcast_fusion, bf16[8,1024]{1,0:T(8,128)(2,1)S(1)} %get-tuple-element.2), kind=kOutput, calls=%fused_computation.14 | convolution fusion | flops 604274688 | bytes 9715712 | tf_op jit(solution)/shard_map/dot_general | solution.py:21
  94.1 49.2 %all-reduce.3 = bf16[72,4096]{1,0:T(8,128)(2,1)S(1)} all-reduce(f32[72,4096]{1,0:T(8,128)S(1)} %fusion.12), channel_id=1, replica_groups=mesh['samp'=8,'snp'=4] {'samp'}, use_global_device_ids=true, to_apply=%region_3.0 | all-reduce | flops 294912 | bytes 1769472 | tf_op jit(solution)/shard_map/psum | solution.py:22
  143.3 6.0 %fusion.26 = f32[72,1024]{1,0:T(8,128)S(1)} fusion(bf16[72,4096]{1,0:T(8,128)(2,1)S(1)} %all-reduce.3, bf16[1024,4096]{1,0:T(8,128)(2,1)} %param.4), kind=kOutput, calls=%fused_computation.35 | convolution fusion | flops 603979776 | bytes 9273344 | tf_op jit(solution)/shard_map/dot_general | solution.py:12
  149.4 1.2 fusion.17
  150.6 15.8 %psum.31 = f32[8,1024]{1,0:T(8,128)S(1)} all-reduce(f32[8,1024]{1,0:T(8,128)S(1)} %fusion.17), channel_id=1, replica_groups=mesh['samp'=8,'snp'=4] {'snp'}, use_global_device_ids=true, to_apply=%region_5.0 | all-reduce | flops 8192 | bytes 65536 | tf_op jit(solution)/shard_map/psum | solution.py:28
  166.4 0.0 copy-done.1
  166.4 1.3 multiply_add_fusion
  (3 shorter events, 0.1 us)
Async XLA Ops:
  8.5 79.8 %copy-start = (bf16[8,1024]{1,0:T(8,128)(2,1)S(1)}, bf16[8,1024]{1,0:T(8,128)(2,1)}, u32[]{:S(2)}) copy-start(bf16[8,1024]{1,0:T(8,128)(2,1)} %param.5) | copy-start | bytes 49156
  89.0 77.4 %copy-start.1 = (f32[8,1024]{1,0:T(8,128)}, f32[8,1024]{1,0:T(8,128)S(1)}, u32[]{:S(2)}) copy-start(f32[8,1024]{1,0:T(8,128)S(1)} %get-tuple-element.3) | copy-start | bytes 98308
where the time goes:
time: 168 us
  blocking collectives  138 us (82%)
  matrix products  22.1 us (13%)
  other arithmetic  5.97 us (4%)
    psum x2, blocking collectives, apply_operator(): snp_panel = lax.psum(partial_panel, 'samp').astype(jnp.bfloat16)  102 us
    psum x2, blocking collectives, apply_operator(): totals = lax.psum(weighted, 'snp')  35.2 us
    dot_general x2, matrix products, local_image(): lax.dot_general(snp_panel, genotypes, (((1,), (1,)), ((), ())), preferred...  12.1 us
    dot_general x2, matrix products, apply_operator(): jnp.dot(panel, genotypes, preferred_element_type=jnp.float32)  9.96 us

commit v1 on v0

--- a/solution.py
+++ b/solution.py
@@ -25,7 +25,7 @@
     blocks = image[PROBES:].reshape(ENVS, PROBES, -1)
     interaction = jnp.sum(onehot.astype(jnp.float32)[:, None, :] * blocks, axis=0)
     weighted = variances[0] * additive / SNPS + variances[1] * interaction / SNPS
-    totals = lax.psum(weighted, "snp")
+    totals = jnp.sum(lax.all_gather(weighted, "snp"), axis=0)
     return totals + variances[2] * current
 
 

time: 168 us -> 157 us (0.935)
  blocking collectives: 138 us -> 130 us
  matrix products: 22.1 us -> 18.9 us
    psum x2 -> x0, blocking collectives: 35.2 us -> none  [apply_operator(): totals = lax.psum(weighted, 'snp')]
    all_gather x0 -> x2, blocking collectives: none -> 27.2 us  [apply_operator(): totals = jnp.sum(lax.all_gather(weighted, 'snp'), axis=0)]
    dot_general x2, matrix products: 9.96 us -> 6.62 us  [apply_operator(): jnp.dot(panel, genotypes, preferred_element_type=jnp.float32)]
where the time goes in v1:
time: 157 us
  blocking collectives  130 us (83%)
  matrix products  18.9 us (12%)
  other arithmetic  5.99 us (4%)
    psum x2, blocking collectives, apply_operator(): snp_panel = lax.psum(partial_panel, 'samp').astype(jnp.bfloat16)  103 us
    all_gather x2, blocking collectives, apply_operator(): totals = jnp.sum(lax.all_gather(weighted, 'snp'), axis=0)  27.2 us
    dot_general x2, matrix products, local_image(): lax.dot_general(snp_panel, genotypes, (((1,), (1,)), ((), ())), preferred...  12.2 us
    dot_general x2, matrix products, apply_operator(): jnp.dot(panel, genotypes, preferred_element_type=jnp.float32)  6.62 us

profile of v1, /device:TPU:0, one launch (start us, length us, event | category | flops | bytes accessed | tf_op | source)
XLA Modules:
  0.0 156.9 jit_solution(8027394821215849512)
XLA Ops:
  0.6 1.4 fusion.25
  2.1 0.7 fusion.21
  2.8 0.7 multiply_bitcast_fusion.1
  3.5 5.0 %fusion.8 = f32[72,4096]{1,0:T(8,128)S(1)} fusion(bf16[1024,4096]{1,0:T(8,128)(2,1)} %param.4, bf16[64,1024]{1,0:T(8,128)(2,1)S(1)} %multiply_bitcast_fusion.1, bf16[8,1024]{1,0:T(8,128)(2,1)} %param.5), kind=kOutput, calls=%fused_computation.10 | convolution fusion | flops 604274688 | bytes 9715712 | tf_op jit(solution)/shard_map/dot_general | solution.py:21
  8.5 0.0 copy-start.1
  8.5 53.0 %all-reduce.2 = bf16[72,4096]{1,0:T(8,128)(2,1)S(1)} all-reduce(f32[72,4096]{1,0:T(8,128)S(1)} %fusion.8), channel_id=1, replica_groups=mesh['samp'=8,'snp'=4] {'samp'}, use_global_device_ids=true, to_apply=%region_0.0 | all-reduce | flops 294912 | bytes 1769472 | tf_op jit(solution)/shard_map/psum | solution.py:22
  61.5 0.0 copy-start
  61.5 6.2 %fusion.27 = f32[72,1024]{1,0:T(8,128)S(1)} fusion(bf16[72,4096]{1,0:T(8,128)(2,1)S(1)} %all-reduce.2, bf16[1024,4096]{1,0:T(8,128)(2,1)} %param.4), kind=kOutput, calls=%fused_computation.38 | convolution fusion | flops 603979776 | bytes 9273344 | tf_op jit(solution)/shard_map/dot_general | solution.py:12
  67.8 1.2 fusion.19
  69.0 13.9 %all-gather = f32[32,1024]{1,0:T(8,128)S(1)} all-gather(f32[8,1024]{1,0:T(8,128)S(1)} %fusion.19), channel_id=2, replica_groups=mesh['samp'=8,'snp'=4] {'snp'}, dimensions={0}, use_global_device_ids=true | all-gather | bytes 163840 | tf_op jit(solution)/shard_map/all_gather | solution.py:28
  82.9 0.0 copy-done.1
  82.9 0.7 fusion.24
  83.6 0.0 copy-start.2
  83.6 0.0 copy-done
  83.7 1.6 %fusion.12 = f32[72,4096]{1,0:T(8,128)S(1)} fusion(bf16[1024,4096]{1,0:T(8,128)(2,1)S(1)} %copy-done, bf16[64,1024]{1,0:T(8,128)(2,1)S(1)} %multiply_bitcast_fusion, bf16[8,1024]{1,0:T(8,128)(2,1)S(1)} %get-tuple-element.2), kind=kOutput, calls=%fused_computation.14 | convolution fusion | flops 604274688 | bytes 9715712 | tf_op jit(solution)/shard_map/dot_general | solution.py:21
  85.3 49.6 %all-reduce.3 = bf16[72,4096]{1,0:T(8,128)(2,1)S(1)} all-reduce(f32[72,4096]{1,0:T(8,128)S(1)} %fusion.12), channel_id=1, replica_groups=mesh['samp'=8,'snp'=4] {'samp'}, use_global_device_ids=true, to_apply=%region_3.0 | all-reduce | flops 294912 | bytes 1769472 | tf_op jit(solution)/shard_map/psum | solution.py:22
  134.9 6.0 %fusion.26 = f32[72,1024]{1,0:T(8,128)S(1)} fusion(bf16[72,4096]{1,0:T(8,128)(2,1)S(1)} %all-reduce.3, bf16[1024,4096]{1,0:T(8,128)(2,1)} %param.4), kind=kOutput, calls=%fused_computation.37 | convolution fusion | flops 603979776 | bytes 9273344 | tf_op jit(solution)/shard_map/dot_general | solution.py:12
  141.0 1.2 fusion.17
  142.2 13.3 %all-gather.1 = f32[32,1024]{1,0:T(8,128)S(1)} all-gather(f32[8,1024]{1,0:T(8,128)S(1)} %fusion.17), channel_id=3, replica_groups=mesh['samp'=8,'snp'=4] {'snp'}, dimensions={0}, use_global_device_ids=true | all-gather | bytes 163840 | tf_op jit(solution)/shard_map/all_gather | solution.py:28
  155.6 0.0 copy-done.2
  155.6 1.3 multiply_add_fusion
  (5 shorter events, 0.1 us)
Async XLA Ops:
  8.5 74.4 %copy-start.1 = (bf16[8,1024]{1,0:T(8,128)(2,1)S(1)}, bf16[8,1024]{1,0:T(8,128)(2,1)}, u32[]{:S(2)}) copy-start(bf16[8,1024]{1,0:T(8,128)(2,1)} %param.5) | copy-start | bytes 49156
  61.5 22.1 %copy-start = (bf16[1024,4096]{1,0:T(8,128)(2,1)S(1)}, bf16[1024,4096]{1,0:T(8,128)(2,1)}, u32[]{:S(2)}) copy-start(bf16[1024,4096]{1,0:T(8,128)(2,1)} %param.4) | copy-start | bytes 25165828
  83.6 72.0 %copy-start.2 = (f32[8,1024]{1,0:T(8,128)}, f32[8,1024]{1,0:T(8,128)S(1)}, u32[]{:S(2)}) copy-start(f32[8,1024]{1,0:T(8,128)S(1)} %get-tuple-element.3) | copy-start | bytes 98308
